TPU v7x, 32 devices: a whole 2x2x4 slice. The times are simulated.
32 devices in a mesh: pr: 8 (over y, x, core), pc: 4 (over z).
Axes of the slice: x: 2, y: 2, z: 4, core: 2. Of those that a mesh axis runs over, the one named last changes fastest.
Arguments:
- pair_array: bfloat16 [256, 256, 128], P('pr', 'pc'), may hold values from -6 to 6
- left_weight: bfloat16 [128, 128], replicated, may hold values from -0.5 to 0.5
- right_weight: bfloat16 [128, 128], replicated, may hold values from -0.5 to 0.5
- left_gate: bfloat16 [128, 128], replicated, may hold values from -0.5 to 0.5
- right_gate: bfloat16 [128, 128], replicated, may hold values from -0.5 to 0.5
- mid_gain: float32 [128], replicated, may hold values from 0.25 to 1.75
- out_weight: bfloat16 [128, 128], replicated, may hold values from -0.5 to 0.5
- out_gate: bfloat16 [128, 128], replicated, may hold values from -0.5 to 0.5
Outputs:
- pair_update: bfloat16 [256, 256, 128], P('pr', 'pc')
All inputs are finite; a program needn't handle non-finite values.
Results may differ from a plain program's by a relative error of at most 0.012.
Values may be sent and summed in bfloat16 or wider, within the bound.
A program may use at most 128 MiB of HBM per device.

v0:
```python
import jax
import jax.numpy as jnp
from jax import lax
from jax.sharding import PartitionSpec as P


def unit_channels(values, channel_gain):
    centred = values - jnp.mean(values, axis=-1, keepdims=True)
    return (
        centred
        * lax.rsqrt(jnp.mean(centred * centred, axis=-1, keepdims=True) + 1e-05)
        * channel_gain
    )


def make_factors(pair_in, left_weight, right_weight, left_gate, right_gate):
    left = jnp.einsum("ijc,cd->ijd", pair_in, left_weight, preferred_element_type=jnp.float32)
    left = left * jax.nn.sigmoid(
        jnp.einsum("ijc,cd->ijd", pair_in, left_gate, preferred_element_type=jnp.float32)
    )
    right = jnp.einsum("ijc,cd->ijd", pair_in, right_weight, preferred_element_type=jnp.float32)
    right = right * jax.nn.sigmoid(
        jnp.einsum("ijc,cd->ijd", pair_in, right_gate, preferred_element_type=jnp.float32)
    )
    return (pair_in, left.astype(jnp.bfloat16), right.astype(jnp.bfloat16))


def to_pair(mixed, ready, mid_gain, out_weight, out_gate):
    scaled = unit_channels(mixed.astype(jnp.float32), mid_gain).astype(jnp.bfloat16)
    scaled = lax.optimization_barrier(scaled)
    gate = jax.nn.sigmoid(
        jnp.einsum("ijc,cd->ijd", ready, out_gate, preferred_element_type=jnp.float32)
    )
    return (
        jnp.einsum("ijd,dc->ijc", scaled, out_weight, preferred_element_type=jnp.float32) * gate
    ).astype(jnp.bfloat16)


def on_device(
    pair_array, left_weight, right_weight, left_gate, right_gate, mid_gain, out_weight, out_gate
):
    ready, left, right = make_factors(pair_array, left_weight, right_weight, left_gate, right_gate)
    count = pair_array.shape[0] * lax.axis_size("pr")
    left_lines, right_lines = (
        lax.all_to_all(left, "pr", split_axis=2, concat_axis=0, tiled=True),
        lax.all_to_all(right, "pr", split_axis=2, concat_axis=0, tiled=True),
    )
    strip = jnp.einsum(
        "kid,kjd->ijd",
        lax.all_gather(left_lines, "pc", axis=1, tiled=True),
        right_lines,
        preferred_element_type=jnp.float32,
    )
    strip = (strip * count ** (-0.5)).astype(jnp.bfloat16)
    mixed = lax.all_to_all(strip, "pr", split_axis=0, concat_axis=2, tiled=True)
    return to_pair(mixed, ready, mid_gain, out_weight, out_gate)


def solution(mesh):
    return jax.shard_map(
        on_device,
        mesh=mesh,
        in_specs=(P("pr", "pc", None), P(), P(), P(), P(), P(), P(), P()),
        out_specs=P("pr", "pc", None),
        check_vma=False,
    )
```

profile of v0, /device:TPU:0, one launch (start us, length us, event | category | flops | bytes accessed | tf_op | source)
XLA Modules:
  0.0 104.0 jit_solution(1541400130074911763)
XLA Ops:
  6.5 1.0 copy-done
  7.6 1.0 fusion.24
  8.6 1.2 %fusion.14 = bf16[32,64,128]{2,1,0:T(8,128)(2,1)S(1)} fusion(f32[32,64,128]{2,1,0:T(8,128)S(1)} %fusion.24, bf16[32,64,128]{2,1,0:T(8,128)(2,1)S(1)} %copy-done, bf16[128,128]{1,0:T(8,128)(2,1)} %param.11), kind=kOutput, calls=%fused_computation.22 | convolution fusion | flops 68419584 | bytes 2129920 | tf_op jit(solution)/shard_map/ijc,cd->ijd/dot_general | solution.py:19
  9.8 1.6 %copy.25 = bf16[32,64,128]{1,0,2:T(8,128)(2,1)S(1)} copy(bf16[32,64,128]{2,1,0:T(8,128)(2,1)S(1)} %fusion.14) | data formatting | bytes 1048576 | tf_op jit(solution)/shard_map/convert_element_type | solution.py:25
  11.4 0.7 reshape.28
  12.2 14.7 %all_to_all.45 = bf16[8,2,16384]{2,1,0:T(2,128)(2,1)S(1)} all-to-all(bf16[8,2,16384]{2,1,0:T(2,128)(2,1)S(1)} %reshape.28), channel_id=1, replica_groups=mesh['pr'=8,'pc'=4] {'pr'}, dimensions={0} | all-to-all | bytes 1048576 | tf_op jit(solution)/shard_map/all_to_all | solution.py:45
  26.8 0.7 reshape.29
  27.5 0.4 copy.27
  28.0 1.6 %copy.28 = bf16[256,64,16]{0,1,2:T(8,128)(2,1)} copy(bf16[256,64,16]{1,2,0:T(8,128)(2,1)S(1)} %bitcast.66) | data formatting | bytes 1048576 | tf_op jit(solution)/shard_map/all_to_all | solution.py:45
  29.9 0.4 fusion.15
  30.4 1.6 %copy.22 = bf16[32,64,128]{1,0,2:T(8,128)(2,1)S(1)} copy(bf16[32,64,128]{2,1,0:T(8,128)(2,1)S(1)} %fusion.15) | data formatting | bytes 1048576 | tf_op jit(solution)/shard_map/convert_element_type | solution.py:25
  32.0 0.7 reshape.30
  32.7 12.1 %all_to_all.46 = bf16[8,2,16384]{2,1,0:T(2,128)(2,1)S(1)} all-to-all(bf16[8,2,16384]{2,1,0:T(2,128)(2,1)S(1)} %reshape.30), channel_id=1, replica_groups=mesh['pr'=8,'pc'=4] {'pr'}, dimensions={0} | all-to-all | bytes 1048576 | tf_op jit(solution)/shard_map/all_to_all | solution.py:46
  44.8 0.7 reshape.31
  45.9 28.9 %all-gather.2.cloned.1.call-done = bf16[256,256,16]{0,1,2:T(8,128)(2,1)} async-done(((bf16[256,64,16]{0,1,2:T(8,128)(2,1)}), bf16[256,256,16]{0,1,2:T(8,128)(2,1)}) %all-gather.2.cloned.1.call-update) | async-done | bytes 2097168 | tf_op jit(solution)/shard_map/all_gather | solution.py:50
  74.8 2.4 %fusion.18 = bf16[256,64,16]{0,1,2:T(8,128)(2,1)S(1)} fusion(bf16[256,256,16]{0,1,2:T(8,128)(2,1)} %all-gather.2.cloned.1.call-done, bf16[256,64,16]{1,2,0:T(8,128)(2,1)S(1)} %bitcast.61), kind=kOutput, calls=%fused_computation.26 | convolution fusion | flops 134742016 | bytes 3145728 | tf_op jit(solution)/shard_map/kid,kjd->ijd/dot_general | solution.py:48
  77.2 1.0 copy.30
  78.1 1.5 %reshape.32 = bf16[8,2,16384]{2,1,0:T(2,128)(2,1)} reshape(bf16[256,16,64]{2,1,0:T(8,128)(2,1)S(1)} %bitcast.64) | data formatting | bytes 1048576
  79.6 3.7 %all-to-all-start.2 = ((bf16[8,2,16384]{2,1,0:T(2,128)(2,1)}), bf16[8,2,16384]{2,1,0:T(2,128)(2,1)S(1)}, u32[]{:S(2)}, u32[]{:S(2)}) async-start(bf16[8,2,16384]{2,1,0:T(2,128)(2,1)} %reshape.32), calls=%async_computation.2 | async-start | bytes 1048576 | tf_op jit(solution)/shard_map/all_to_all | solution.py:55
  83.3 0.4 fusion.13
  83.8 9.3 %all-to-all-done.2 = bf16[8,2,16384]{2,1,0:T(2,128)(2,1)S(1)} async-done(((bf16[8,2,16384]{2,1,0:T(2,128)(2,1)}), bf16[8,2,16384]{2,1,0:T(2,128)(2,1)S(1)}, u32[]{:S(2)}, u32[]{:S(2)}) %all-to-all-start.2) | async-done | bytes 524320 | tf_op jit(solution)/shard_map/all_to_all | solution.py:55
  93.0 0.7 reshape.33
  95.2 0.5 fusion.2
  95.9 1.3 %fusion.17 = bf16[32,64,128]{2,1,0:T(8,128)(2,1)} fusion(f32[32,64,128]{2,1,0:T(8,128)S(1)} %fusion.13, bf16[32,64,128]{1,2,0:T(8,128)(2,1)S(1)} %fusion.2, bf16[128,128]{1,0:T(8,128)(2,1)S(1)} %copy-done.2), kind=kOutput, calls=%fused_computation.25 | convolution fusion | flops 67633152 | bytes 2129920 | tf_op jit(solution)/shard_map/ijd,dc->ijc/dot_general | solution.py:35
  (21 shorter events, 2.5 us)
Async XLA Ops:
  6.5 1.0 %copy-start = (bf16[32,64,128]{2,1,0:T(8,128)(2,1)S(1)}, bf16[32,64,128]{2,1,0:T(8,128)(2,1)}, u32[]{:S(2)}) copy-start(bf16[32,64,128]{2,1,0:T(8,128)(2,1)} %param.8) | copy-start | bytes 1572868
  6.5 68.3 %all-gather.2.cloned.1.call-start = ((), (), s32[]{:S(2)}) async-start(), calls=%async_computation.3 | async-start | bytes 2621440 | tf_op jit(solution)/shard_map/all_gather | solution.py:50
  27.5 2.1 %copy-start.1 = (bf16[128,128]{1,0:T(8,128)(2,1)S(1)}, bf16[128,128]{1,0:T(8,128)(2,1)}, u32[]{:S(2)}) copy-start(bf16[128,128]{1,0:T(8,128)(2,1)} %param.10) | copy-start | bytes 98308
  27.9 2.0 %copy-start.4 = (bf16[128,128]{1,0:T(8,128)(2,1)S(1)}, bf16[128,128]{1,0:T(8,128)(2,1)}, u32[]{:S(2)}) copy-start(bf16[128,128]{1,0:T(8,128)(2,1)} %param.12) | copy-start | bytes 98308
  77.2 6.2 %copy-start.5 = (bf16[128,128]{1,0:T(8,128)(2,1)S(1)}, bf16[128,128]{1,0:T(8,128)(2,1)}, u32[]{:S(2)}) copy-start(bf16[128,128]{1,0:T(8,128)(2,1)} %param.15) | copy-start | bytes 98308
  79.6 13.4 %all-to-all-start.2 = ((bf16[8,2,16384]{2,1,0:T(2,128)(2,1)}), bf16[8,2,16384]{2,1,0:T(2,128)(2,1)S(1)}, u32[]{:S(2)}, u32[]{:S(2)}) async-start(bf16[8,2,16384]{2,1,0:T(2,128)(2,1)} %reshape.32), calls=%async_computation.2 | async-start | bytes 1048576 | tf_op jit(solution)/shard_map/all_to_all | solution.py:55
  94.5 0.7 copy-start.3
  95.2 0.8 copy-start.2
Sparse Core Ops, SparseCore 0:
  29.7 45.0 all-gather.1
where the time goes:
time: 105 us; the launch traced here: 104 us
  waiting for transfers between devices  38.2 us (36%)
  blocking collectives  26.8 us (26%)
  between operations  13.6 us (13%)
  local copies, waits for them, and re-layouts  13.5 us (13%)
  matrix products  6.96 us (7%)
  starting transfers between devices  3.68 us (4%)
  other arithmetic  1.27 us (1%)
    all_gather x1, waiting for transfers between devices, on_device(): lax.all_gather(left_lines, 'pc', axis=1, tiled=True)  28.9 us
    all_to_all x1, blocking collectives, on_device(): lax.all_to_all(left, 'pr', split_axis=2, concat_axis=0, tiled=True)  14.7 us
    all_to_all x1, blocking collectives, on_device(): lax.all_to_all(right, 'pr', split_axis=2, concat_axis=0, tiled=True)  12.1 us
    all_to_all x1, waiting for transfers between devices, on_device(): mixed = lax.all_to_all(strip, 'pr', split_axis=0, concat_axis=2, tiled=True)  9.25 us
    unnamed x18, local copies, waits for them, and re-layouts  6.59 us
    all_to_all x1, starting transfers between devices, on_device(): mixed = lax.all_to_all(strip, 'pr', split_axis=0, concat_axis=2, tiled=True)  3.67 us
    convert_element_type x2, local copies, waits for them, and re-layouts, make_factors(): return (pair_in, left.astype(jnp.bfloat16), right.astype(jnp.bfloat16))  3.24 us
    dot_general x1, matrix products, on_device(): jnp.einsum('kid,kjd->ijd', lax.all_gather(left_lines, 'pc', axis=1, tiled...  2.35 us
  transfers between devices with their start and end apart: 2, of which 2 were waited for; matrix products, arithmetic and copies ran while one was open for 4% of the time, Pallas kernels for 0%

commit v1 on v0

v1 whole, which is shorter than its diff:
```python
import functools

import jax
import jax.numpy as jnp
from jax import lax
from jax.experimental import pallas as pl
from jax.experimental.pallas import tpu as pltpu
from jax.sharding import PartitionSpec as P

MESH = pl.DeviceIdType.MESH
BF16 = jnp.bfloat16
F32 = jnp.float32
LANES = 128
SUB = 16


def unit_channels(values, channel_gain):
    centred = values - jnp.mean(values, axis=-1, keepdims=True)
    return (
        centred
        * lax.rsqrt(jnp.mean(centred * centred, axis=-1, keepdims=True) + 1e-05)
        * channel_gain
    )


def make_factors(pair_in, left_weight, right_weight, left_gate, right_gate):
    left = jnp.einsum("ijc,cd->ijd", pair_in, left_weight, preferred_element_type=F32)
    left = left * jax.nn.sigmoid(
        jnp.einsum("ijc,cd->ijd", pair_in, left_gate, preferred_element_type=F32)
    )
    right = jnp.einsum("ijc,cd->ijd", pair_in, right_weight, preferred_element_type=F32)
    right = right * jax.nn.sigmoid(
        jnp.einsum("ijc,cd->ijd", pair_in, right_gate, preferred_element_type=F32)
    )
    return (pair_in, left.astype(BF16), right.astype(BF16))


def to_pair(mixed, ready, mid_gain, out_weight, out_gate):
    scaled = unit_channels(mixed.astype(F32), mid_gain).astype(BF16)
    scaled = lax.optimization_barrier(scaled)
    gate = jax.nn.sigmoid(jnp.einsum("ijc,cd->ijd", ready, out_gate, preferred_element_type=F32))
    return (
        jnp.einsum("ijd,dc->ijc", scaled, out_weight, preferred_element_type=F32) * gate
    ).astype(BF16)


def plain(
    pair_array, left_weight, right_weight, left_gate, right_gate, mid_gain, out_weight, out_gate
):
    ready, left, right = make_factors(pair_array, left_weight, right_weight, left_gate, right_gate)
    count = pair_array.shape[0] * lax.axis_size("pr")
    left_lines, right_lines = (
        lax.all_to_all(left, "pr", split_axis=2, concat_axis=0, tiled=True),
        lax.all_to_all(right, "pr", split_axis=2, concat_axis=0, tiled=True),
    )
    strip = jnp.einsum(
        "kid,kjd->ijd",
        lax.all_gather(left_lines, "pc", axis=1, tiled=True),
        right_lines,
        preferred_element_type=F32,
    )
    strip = (strip * count ** (-0.5)).astype(BF16)
    mixed = lax.all_to_all(strip, "pr", split_axis=0, concat_axis=2, tiled=True)
    return to_pair(mixed, ready, mid_gain, out_weight, out_gate)


def nt(a, b):
    return lax.dot_general(a, b, (((1,), (1,)), ((), ())), preferred_element_type=F32)


def tn(a, b):
    return lax.dot_general(a, b, (((0,), (0,)), ((), ())), preferred_element_type=F32)


GROUPS = ((0, 0), (0, 1), (1, 0), (1, 1))


def kernel(
    n_p, n_q, x_ref, lw_ref, rw_ref, lg_ref, rg_ref, gain_ref, ow_ref, og_ref, out_ref,
    turn, lsend, rsend, lrecv, rrecv, osend, orecv, gate,
    l_ss, l_rs, r_ss, r_rs, o_ss, o_rs,
):
    p = lax.axis_index("pr")
    q = lax.axis_index("pc")
    zh = q // 2
    zl = q % 2
    me = p * 2 + zl
    n_e = n_p * 2
    per = lsend.shape[1] // SUB
    width = x_ref.shape[1]
    rows = x_ref.shape[0] // 2
    channels = n_e * per
    count = n_p * x_ref.shape[0]

    barrier = pltpu.get_barrier_semaphore()
    for dp in range(n_p):
        for dh, dl in GROUPS:
            if (dp, dh, dl) != (0, 0, 0):
                to = (lax.rem(p + dp, n_p), lax.rem(zh + dh, 2) * 2 + lax.rem(zl + dl, 2))
                pl.semaphore_signal(barrier, inc=1, device_id=to, device_id_type=MESH)

    def pair_rows(k):
        return jnp.concatenate([x_ref[k], x_ref[k + rows]], axis=0)

    def factor(w_ref, g_ref, send):
        both = jnp.concatenate([w_ref[...].T, g_ref[...].T], axis=0)

        def step(k, _):
            pr = nt(both, pair_rows(k))
            turn[pl.ds(k, channels, stride=SUB), :] = pr[:channels] * jax.nn.sigmoid(pr[channels:])
            return 0

        lax.fori_loop(0, rows, step, 0, unroll=2)

        def cast(e, _):
            at = pl.multiple_of(e * per * SUB, per * SUB)
            send[e] = turn[pl.ds(at, per * SUB), :].astype(BF16)
            return 0

        lax.fori_loop(0, n_e, cast, 0)

    def r_copy(dp, dl, arriving=False):
        to_p, to_l = lax.rem(p + dp, n_p), lax.rem(zl + dl, 2)
        return pltpu.make_async_remote_copy(
            src_ref=rsend.at[to_p * 2 + to_l],
            dst_ref=rrecv.at[dl, dp],
            send_sem=r_ss.at[dl, dp],
            recv_sem=r_rs.at[dl, dp],
            device_id=(to_p, zh * 2 + to_l),
            device_id_type=MESH,
        )

    def l_copy(dp, group):
        dh, dl = GROUPS[group]
        to_p, to_l = lax.rem(p + dp, n_p), lax.rem(zl + dl, 2)
        return pltpu.make_async_remote_copy(
            src_ref=lsend.at[to_p * 2 + to_l],
            dst_ref=lrecv.at[group, dp],
            send_sem=l_ss.at[group, dp],
            recv_sem=l_rs.at[group, dp],
            device_id=(to_p, lax.rem(zh + dh, 2) * 2 + to_l),
            device_id_type=MESH,
        )

    factor(rw_ref, rg_ref, rsend)
    pl.semaphore_wait(barrier, n_p * n_q - 1)
    for dl in (1, 0):
        for dp in range(n_p):
            if (dp, dl) != (0, 0):
                r_copy(dp, dl).start()
    factor(lw_ref, lg_ref, lsend)
    for group in range(4):
        for dp in range(n_p):
            if (dp, group) != (0, 0):
                l_copy(dp, group).start()
    rrecv[0, 0] = rsend[me]
    lrecv[0, 0] = lsend[me]

    def make_gate(k, _):
        gate[k] = jax.nn.sigmoid(
            jnp.dot(pair_rows(k), og_ref[...], preferred_element_type=F32)
        )
        return 0

    lax.fori_loop(0, rows, make_gate, 0)

    for dl in (1, 0):
        for dp in range(n_p):
            if (dp, dl) != (0, 0):
                r_copy(dp, dl).wait_recv()

    low = lax.broadcasted_iota(jnp.int32, (SUB, LANES), 1) < width

    def o_copy(group, b, dl):
        dh, gl = GROUPS[group]
        z = lax.rem(zh + dh, 2) * 2 + lax.rem(zl + gl, 2)
        to_p, to_l = z * 2 + b, lax.rem(zl + dl, 2)
        away = (to_p != p) if dl == 0 else None
        return away, pltpu.make_async_remote_copy(
            src_ref=osend.at[group, b, dl],
            dst_ref=orecv.at[me],
            send_sem=o_ss.at[group, b, dl],
            recv_sem=o_rs.at[me],
            device_id=(to_p, zh * 2 + to_l),
            device_id_type=MESH,
        )

    for group in range(4):
        for dp in range(n_p):
            if (dp, group) != (0, 0):
                l_copy(dp, group).wait_recv()

        def products(d, _):
            at = pl.ds(pl.multiple_of(d * SUB, SUB), SUB)
            left = lrecv[group, :, at, :].reshape(n_p * SUB, LANES)
            for dl in range(2):
                right = rrecv[dl, :, at, :].reshape(n_p * SUB, LANES)
                acc = tn(left, right)
                for b in range(2):
                    top = b * 2 * SUB
                    a0, c0 = acc[top : top + SUB], acc[top + SUB : top + 2 * SUB]
                    b0 = acc[width + top : width + top + SUB]
                    d0 = acc[width + top + SUB : width + top + 2 * SUB]
                    tile = jnp.where(low, a0, d0) + pltpu.roll(
                        jnp.where(low, c0, b0), width, 1
                    )
                    osend[group, b, dl, at, :] = (tile * count ** (-0.5)).astype(BF16)
            return 0

        lax.fori_loop(0, per, products, 0, unroll=2)
        for b in range(2):
            for dl in (1, 0):
                away, copy = o_copy(group, b, dl)
                if away is None:
                    copy.start()
                else:

                    @pl.when(away)
                    def _():
                        copy.start()

                    @pl.when(jnp.logical_not(away))
                    def _():
                        orecv[me] = osend[group, b, dl]

    gain = jnp.broadcast_to(gain_ref[...], (channels, channels)).T
    for off in range(1, n_e):
        at = lax.rem(me + off, n_e)
        pltpu.make_async_remote_copy(
            src_ref=osend.at[0, 0, 0],
            dst_ref=orecv.at[at],
            send_sem=o_ss.at[0, 0, 0],
            recv_sem=o_rs.at[at],
            device_id=(p, q),
            device_id_type=MESH,
        ).wait_recv()

    def widen(e, _):
        at = pl.multiple_of(e * per * SUB, per * SUB)
        turn[pl.ds(at, per * SUB), :] = orecv[e].astype(F32)
        return 0

    lax.fori_loop(0, n_e, widen, 0)

    def finish(k, _):
        v = turn[pl.ds(k, channels, stride=SUB), :]
        v = v - jnp.mean(v, axis=0, keepdims=True)
        v = v * lax.rsqrt(jnp.mean(v * v, axis=0, keepdims=True) + 1e-05) * gain
        res = (tn(v.astype(BF16), ow_ref[...]) * gate[k]).astype(BF16)
        out_ref[k] = res[:width]
        out_ref[k + rows] = res[width:]
        return 0

    lax.fori_loop(0, rows, finish, 0, unroll=2)

    for dl in range(2):
        for dp in range(n_p):
            if (dp, dl) != (0, 0):
                r_copy(dp, dl).wait_send()
    for group in range(4):
        for dp in range(n_p):
            if (dp, group) != (0, 0):
                l_copy(dp, group).wait_send()
        for b in range(2):
            for dl in range(2):
                away, copy = o_copy(group, b, dl)
                if away is None:
                    copy.wait_send()
                else:

                    @pl.when(away)
                    def _():
                        copy.wait_send()


def fused(n_p, n_q, pair_array, lw, rw, lg, rg, gain, ow, og):
    channels = lw.shape[1]
    n_e = n_p * 2
    slab = channels // n_e * SUB
    rows = pair_array.shape[0] // 2
    dma = pltpu.SemaphoreType.DMA
    return pl.pallas_call(
        functools.partial(kernel, n_p, n_q),
        out_shape=jax.ShapeDtypeStruct(pair_array.shape, BF16),
        in_specs=[pl.BlockSpec(memory_space=pltpu.VMEM)] * 8,
        out_specs=pl.BlockSpec(memory_space=pltpu.VMEM),
        scratch_shapes=[
            pltpu.VMEM((channels * SUB, LANES), F32),
            pltpu.VMEM((n_e, slab, LANES), BF16),
            pltpu.VMEM((n_e, slab, LANES), BF16),
            pltpu.VMEM((4, n_p, slab, LANES), BF16),
            pltpu.VMEM((2, n_p, slab, LANES), BF16),
            pltpu.VMEM((4, 2, 2, slab, LANES), BF16),
            pltpu.VMEM((n_e, slab, LANES), BF16),
            pltpu.VMEM((rows, LANES, channels), F32),
            dma((4, n_p)),
            dma((4, n_p)),
            dma((2, n_p)),
            dma((2, n_p)),
            dma((4, 2, 2)),
            dma((n_e,)),
        ],
        compiler_params=pltpu.CompilerParams(
            collective_id=0, has_side_effects=True, vmem_limit_bytes=40 * 2**20
        ),
    )(pair_array, lw, rw, lg, rg, gain.reshape(1, channels), ow, og)


def solution(mesh):
    n_p, n_q = mesh.shape["pr"], mesh.shape["pc"]

    def on_device(pair_array, lw, *rest):
        first, second, wide = pair_array.shape
        fits = (
            n_q == 4
            and first == 2 * SUB
            and second == 2 * first
            and n_p == 2 * n_q
            and 2 * second == LANES
            and wide == LANES
            and lw.shape[1] == LANES
        )
        if fits:
            return fused(n_p, n_q, pair_array, lw, *rest)
        return plain(pair_array, lw, *rest)

    return jax.shard_map(
        on_device,
        mesh=mesh,
        in_specs=(P("pr", "pc", None), P(), P(), P(), P(), P(), P(), P()),
        out_specs=P("pr", "pc", None),
        check_vma=False,
    )
```

time: 105 us -> 48.7 us (0.46)
  the two profiles are of different devices: /device:TPU:0 before, /device:TPU:7 now
where the time goes in v1:
time: 48.7 us; the launch traced here: 47.9 us
  Pallas kernels  40.9 us (84%)
  local copies, waits for them, and re-layouts  7.04 us (14%)
    pallas_call x1, Pallas kernels, fused(): pl.pallas_call(functools.partial(kernel, n_p, n_q), out_shape=jax.ShapeDt...  40.9 us
    unnamed x17, local copies, waits for them, and re-layouts  7.04 us

profile of v1, /device:TPU:7, one launch (start us, length us, event | category | flops | bytes accessed | tf_op | source)
XLA Modules:
  0.0 47.9 jit_solution(1685131231291757322)
XLA Ops:
  0.0 0.0 copy-start.7
  0.0 0.7 %copy-done.7 = f32[128]{0:T(128)S(1)} copy-done((f32[128]{0:T(128)S(1)}, f32[128]{0:T(128)}, u32[]{:S(2)}) %copy-start.7) | copy-done | bytes 536
  0.7 0.0 copy-start
  0.7 1.0 %copy-done = bf16[32,64,128]{2,1,0:T(8,128)(2,1)S(1)} copy-done((bf16[32,64,128]{2,1,0:T(8,128)(2,1)S(1)}, bf16[32,64,128]{2,1,0:T(8,128)(2,1)}, u32[]{:S(2)}) %copy-start) | copy-done | bytes 524312
  1.7 0.0 copy-start.1
  1.7 0.8 %copy-done.1 = bf16[128,128]{1,0:T(8,128)(2,1)S(1)} copy-done((bf16[128,128]{1,0:T(8,128)(2,1)S(1)}, bf16[128,128]{1,0:T(8,128)(2,1)}, u32[]{:S(2)}) %copy-start.1) | copy-done | bytes 32792
  2.5 0.0 copy-start.2
  2.5 0.8 %copy-done.2 = bf16[128,128]{1,0:T(8,128)(2,1)S(1)} copy-done((bf16[128,128]{1,0:T(8,128)(2,1)S(1)}, bf16[128,128]{1,0:T(8,128)(2,1)}, u32[]{:S(2)}) %copy-start.2) | copy-done | bytes 32792
  3.2 0.0 copy-start.3
  3.2 0.8 %copy-done.3 = bf16[128,128]{1,0:T(8,128)(2,1)S(1)} copy-done((bf16[128,128]{1,0:T(8,128)(2,1)S(1)}, bf16[128,128]{1,0:T(8,128)(2,1)}, u32[]{:S(2)}) %copy-start.3) | copy-done | bytes 32792
  4.0 0.0 copy-start.4
  4.0 0.8 %copy-done.4 = bf16[128,128]{1,0:T(8,128)(2,1)S(1)} copy-done((bf16[128,128]{1,0:T(8,128)(2,1)S(1)}, bf16[128,128]{1,0:T(8,128)(2,1)}, u32[]{:S(2)}) %copy-start.4) | copy-done | bytes 32792
  4.7 0.0 copy-start.5
  4.7 0.8 %copy-done.5 = bf16[128,128]{1,0:T(8,128)(2,1)S(1)} copy-done((bf16[128,128]{1,0:T(8,128)(2,1)S(1)}, bf16[128,128]{1,0:T(8,128)(2,1)}, u32[]{:S(2)}) %copy-start.5) | copy-done | bytes 32792
  5.5 0.0 copy-start.6
  5.5 0.8 %copy-done.6 = bf16[128,128]{1,0:T(8,128)(2,1)S(1)} copy-done((bf16[128,128]{1,0:T(8,128)(2,1)S(1)}, bf16[128,128]{1,0:T(8,128)(2,1)}, u32[]{:S(2)}) %copy-start.6) | copy-done | bytes 32792
  6.2 40.9 %shard_map.82 = bf16[32,64,128]{2,1,0:T(8,128)(2,1)S(1)} custom-call(bf16[32,64,128]{2,1,0:T(8,128)(2,1)S(1)} %copy-done, bf16[128,128]{1,0:T(8,128)(2,1)S(1)} %copy-done.1, bf16[128,128]{1,0:T(8,128)(2,1)S(1)} %copy-done.2, bf16[128,128]{1,0:T(8,128)(2,1)S(1)} %copy-done.3, bf16[128,128]{1,0:T(8,128)(2,1)S(1)} %copy-done.4, f32[1,128]{1,0:T(1,128)S(1)} %bitcast.1, ...), custom_call_target="tpu_custom_call" | custom-call | tf_op jit(solution)/shard_map/pallas_call | solution.py:282
  47.1 0.8 %copy.10 = bf16[32,64,128]{2,1,0:T(8,128)(2,1)} copy(bf16[32,64,128]{2,1,0:T(8,128)(2,1)S(1)} %shard_map.82) | data formatting | bytes 1048576
Async XLA Ops:
  0.0 0.7 %copy-start.7 = (f32[128]{0:T(128)S(1)}, f32[128]{0:T(128)}, u32[]{:S(2)}) copy-start(f32[128]{0:T(128)} %param.13) | copy-start | bytes 1540
  0.7 1.0 %copy-start = (bf16[32,64,128]{2,1,0:T(8,128)(2,1)S(1)}, bf16[32,64,128]{2,1,0:T(8,128)(2,1)}, u32[]{:S(2)}) copy-start(bf16[32,64,128]{2,1,0:T(8,128)(2,1)} %x_ref.1) | copy-start | bytes 1572868
  1.7 0.8 %copy-start.1 = (bf16[128,128]{1,0:T(8,128)(2,1)S(1)}, bf16[128,128]{1,0:T(8,128)(2,1)}, u32[]{:S(2)}) copy-start(bf16[128,128]{1,0:T(8,128)(2,1)} %lw_ref.1) | copy-start | bytes 98308
  2.5 0.8 %copy-start.2 = (bf16[128,128]{1,0:T(8,128)(2,1)S(1)}, bf16[128,128]{1,0:T(8,128)(2,1)}, u32[]{:S(2)}) copy-start(bf16[128,128]{1,0:T(8,128)(2,1)} %rw_ref.1) | copy-start | bytes 98308
  3.2 0.8 %copy-start.3 = (bf16[128,128]{1,0:T(8,128)(2,1)S(1)}, bf16[128,128]{1,0:T(8,128)(2,1)}, u32[]{:S(2)}) copy-start(bf16[128,128]{1,0:T(8,128)(2,1)} %lg_ref.1) | copy-start | bytes 98308
  4.0 0.8 %copy-start.4 = (bf16[128,128]{1,0:T(8,128)(2,1)S(1)}, bf16[128,128]{1,0:T(8,128)(2,1)}, u32[]{:S(2)}) copy-start(bf16[128,128]{1,0:T(8,128)(2,1)} %rg_ref.1) | copy-start | bytes 98308
  4.7 0.8 %copy-start.5 = (bf16[128,128]{1,0:T(8,128)(2,1)S(1)}, bf16[128,128]{1,0:T(8,128)(2,1)}, u32[]{:S(2)}) copy-start(bf16[128,128]{1,0:T(8,128)(2,1)} %ow_ref.1) | copy-start | bytes 98308
  5.5 0.8 %copy-start.6 = (bf16[128,128]{1,0:T(8,128)(2,1)S(1)}, bf16[128,128]{1,0:T(8,128)(2,1)}, u32[]{:S(2)}) copy-start(bf16[128,128]{1,0:T(8,128)(2,1)} %og_ref.1) | copy-start | bytes 98308

commit v2 on v1

--- a/solution.py
+++ b/solution.py
@@ -12,6 +12,7 @@
 F32 = jnp.float32
 LANES = 128
 SUB = 16
+UF, UP, UE = 16, 8, 16
 
 
 def unit_channels(values, channel_gain):
@@ -76,7 +77,8 @@
 
 
 def kernel(
-    n_p, n_q, x_ref, lw_ref, rw_ref, lg_ref, rg_ref, gain_ref, ow_ref, og_ref, out_ref,
+    n_p, n_q, x_hbm, lw_hbm, rw_hbm, lg_hbm, rg_hbm, gain_hbm, ow_hbm, og_hbm, out_ref,
+    x_ref, lw_ref, rw_ref, lg_ref, rg_ref, gain_ref, ow_ref, og_ref, in_s,
     turn, lsend, rsend, lrecv, rrecv, osend, orecv, gate,
     l_ss, l_rs, r_ss, r_rs, o_ss, o_rs,
 ):
@@ -92,6 +94,18 @@
     channels = n_e * per
     count = n_p * x_ref.shape[0]
 
+    brought = [
+        pltpu.make_async_copy(src, dst, in_s.at[at])
+        for at, (src, dst) in enumerate(
+            (
+                (x_hbm, x_ref), (rw_hbm, rw_ref), (rg_hbm, rg_ref), (lw_hbm, lw_ref),
+                (lg_hbm, lg_ref), (og_hbm, og_ref), (ow_hbm, ow_ref), (gain_hbm, gain_ref),
+            )
+        )
+    ]
+    for copy in brought:
+        copy.start()
+
     barrier = pltpu.get_barrier_semaphore()
     for dp in range(n_p):
         for dh, dl in GROUPS:
@@ -110,14 +124,14 @@
             turn[pl.ds(k, channels, stride=SUB), :] = pr[:channels] * jax.nn.sigmoid(pr[channels:])
             return 0
 
-        lax.fori_loop(0, rows, step, 0, unroll=2)
+        lax.fori_loop(0, rows, step, 0, unroll=UF)
 
         def cast(e, _):
             at = pl.multiple_of(e * per * SUB, per * SUB)
             send[e] = turn[pl.ds(at, per * SUB), :].astype(BF16)
             return 0
 
-        lax.fori_loop(0, n_e, cast, 0)
+        lax.fori_loop(0, n_e, cast, 0, unroll=4)
 
     def r_copy(dp, dl, arriving=False):
         to_p, to_l = lax.rem(p + dp, n_p), lax.rem(zl + dl, 2)
@@ -142,6 +156,8 @@
             device_id_type=MESH,
         )
 
+    for copy in brought:
+        copy.wait()
     factor(rw_ref, rg_ref, rsend)
     pl.semaphore_wait(barrier, n_p * n_q - 1)
     for dl in (1, 0):
@@ -162,7 +178,7 @@
         )
         return 0
 
-    lax.fori_loop(0, rows, make_gate, 0)
+    lax.fori_loop(0, rows, make_gate, 0, unroll=4)
 
     for dl in (1, 0):
         for dp in range(n_p):
@@ -193,9 +209,10 @@
         def products(d, _):
             at = pl.ds(pl.multiple_of(d * SUB, SUB), SUB)
             left = lrecv[group, :, at, :].reshape(n_p * SUB, LANES)
+            right = [rrecv[dl, :, at, :].reshape(n_p * SUB, LANES) for dl in range(2)]
+            sums = tn(left, jnp.concatenate(right, axis=1))
             for dl in range(2):
-                right = rrecv[dl, :, at, :].reshape(n_p * SUB, LANES)
-                acc = tn(left, right)
+                acc = sums[:, dl * LANES : (dl + 1) * LANES]
                 for b in range(2):
                     top = b * 2 * SUB
                     a0, c0 = acc[top : top + SUB], acc[top + SUB : top + 2 * SUB]
@@ -207,7 +224,7 @@
                     osend[group, b, dl, at, :] = (tile * count ** (-0.5)).astype(BF16)
             return 0
 
-        lax.fori_loop(0, per, products, 0, unroll=2)
+        lax.fori_loop(0, per, products, 0, unroll=UP)
         for b in range(2):
             for dl in (1, 0):
                 away, copy = o_copy(group, b, dl)
@@ -240,7 +257,7 @@
         turn[pl.ds(at, per * SUB), :] = orecv[e].astype(F32)
         return 0
 
-    lax.fori_loop(0, n_e, widen, 0)
+    lax.fori_loop(0, n_e, widen, 0, unroll=4)
 
     def finish(k, _):
         v = turn[pl.ds(k, channels, stride=SUB), :]
@@ -251,7 +268,7 @@
         out_ref[k + rows] = res[width:]
         return 0
 
-    lax.fori_loop(0, rows, finish, 0, unroll=2)
+    lax.fori_loop(0, rows, finish, 0, unroll=UE)
 
     for dl in range(2):
         for dp in range(n_p):
@@ -282,9 +299,15 @@
     return pl.pallas_call(
         functools.partial(kernel, n_p, n_q),
         out_shape=jax.ShapeDtypeStruct(pair_array.shape, BF16),
-        in_specs=[pl.BlockSpec(memory_space=pltpu.VMEM)] * 8,
+        in_specs=[pl.BlockSpec(memory_space=pltpu.HBM)] * 8,
         out_specs=pl.BlockSpec(memory_space=pltpu.VMEM),
         scratch_shapes=[
+            pltpu.VMEM(pair_array.shape, BF16),
+            *[pltpu.VMEM(lw.shape, BF16)] * 4,
+            pltpu.VMEM((1, channels), F32),
+            pltpu.VMEM(ow.shape, BF16),
+            pltpu.VMEM(og.shape, BF16),
+            dma((8,)),
             pltpu.VMEM((channels * SUB, LANES), F32),
             pltpu.VMEM((n_e, slab, LANES), BF16),
             pltpu.VMEM((n_e, slab, LANES), BF16),
@@ -301,7 +324,7 @@
             dma((n_e,)),
         ],
         compiler_params=pltpu.CompilerParams(
-            collective_id=0, has_side_effects=True, vmem_limit_bytes=40 * 2**20
+            collective_id=0, has_side_effects=True, vmem_limit_bytes=67_043_328
         ),
     )(pair_array, lw, rw, lg, rg, gain.reshape(1, channels), ow, og)
 

time: 48.7 us -> 42.2 us (0.87); the launches traced: 47.9 us -> 42.1 us
  local copies, waits for them, and re-layouts: 7.04 us -> 1.87 us
  Pallas kernels: 40.9 us -> 40.2 us
    unnamed x17 -> x1, local copies, waits for them, and re-layouts: 7.04 us -> 1.87 us
    pallas_call x1, Pallas kernels: 40.9 us -> 40.2 us  [fused(): pl.pallas_call(functools.partial(kernel, n_p, n_q), out_shape=jax.ShapeDt...]
where the time goes in v2:
time: 42.2 us; the launch traced here: 42.1 us
  Pallas kernels  40.2 us (95%)
  local copies, waits for them, and re-layouts  1.87 us (4%)
    pallas_call x1, Pallas kernels, fused(): pl.pallas_call(functools.partial(kernel, n_p, n_q), out_shape=jax.ShapeDt...  40.2 us
    unnamed x1, local copies, waits for them, and re-layouts  1.87 us

profile of v2, /device:TPU:7, one launch (start us, length us, event | category | flops | bytes accessed | tf_op | source)
XLA Modules:
  0.0 42.1 jit_solution(7699986066489069951)
XLA Ops:
  0.0 40.2 %shard_map.82 = bf16[32,64,128]{2,1,0:T(8,128)(2,1)} custom-call(bf16[32,64,128]{2,1,0:T(8,128)(2,1)} %x_hbm.1, bf16[128,128]{1,0:T(8,128)(2,1)} %lw_hbm.1, bf16[128,128]{1,0:T(8,128)(2,1)} %rw_hbm.1, bf16[128,128]{1,0:T(8,128)(2,1)} %lg_hbm.1, bf16[128,128]{1,0:T(8,128)(2,1)} %rg_hbm.1, f32[1,128]{1,0:T(1,128)} %bitcast.1, bf16[128,128]{1,0:T(8,128)(2,1)} %ow_hbm.1, ...), custom_call_target="tpu_custom_call" | custom-call | tf_op jit(solution)/shard_map/pallas_call | solution.py:299
  40.2 1.9 %copy.10 = bf16[32,64,128]{2,1,0:T(8,128)(2,1)} copy(bf16[32,64,128]{2,1,0:T(8,128)(2,1)} %shard_map.82) | data formatting | bytes 1048576

commit v3 on v2

--- a/solution.py
+++ b/solution.py
@@ -73,26 +73,32 @@
     return lax.dot_general(a, b, (((0,), (0,)), ((), ())), preferred_element_type=F32)
 
 
-GROUPS = ((0, 0), (0, 1), (1, 0), (1, 1))
-
-
 def kernel(
     n_p, n_q, x_hbm, lw_hbm, rw_hbm, lg_hbm, rg_hbm, gain_hbm, ow_hbm, og_hbm, out_ref,
     x_ref, lw_ref, rw_ref, lg_ref, rg_ref, gain_ref, ow_ref, og_ref, in_s,
     turn, lsend, rsend, lrecv, rrecv, osend, orecv, gate,
-    l_ss, l_rs, r_ss, r_rs, o_ss, o_rs,
+    l_ss, l_rs, r_ss, r_rs, lf_ss, lf_rs, rf_ss, rf_rs, o_ss, o_rs,
 ):
     p = lax.axis_index("pr")
     q = lax.axis_index("pc")
-    zh = q // 2
-    zl = q % 2
-    me = p * 2 + zl
-    n_e = n_p * 2
+    half = q // 2
+    is_inner = lax.rem(half + q, 2) == 1
+    inner, end = 1 + half, 3 * half
+    partner = half * 2 + 1 - lax.rem(q, 2)
+    across = 2 - half
+    other_end = 3 - end
     per = lsend.shape[1] // SUB
     width = x_ref.shape[1]
     rows = x_ref.shape[0] // 2
-    channels = n_e * per
+    channels = n_p * per
     count = n_p * x_ref.shape[0]
+
+    def peer(m):
+        bits, to, scale = m, 0, 1
+        while scale < n_p:
+            to = to + lax.rem(p // scale + bits % 2, 2) * scale
+            bits, scale = bits // 2, scale * 2
+        return to
 
     brought = [
         pltpu.make_async_copy(src, dst, in_s.at[at])
@@ -107,10 +113,10 @@
         copy.start()
 
     barrier = pltpu.get_barrier_semaphore()
-    for dp in range(n_p):
-        for dh, dl in GROUPS:
-            if (dp, dh, dl) != (0, 0, 0):
-                to = (lax.rem(p + dp, n_p), lax.rem(zh + dh, 2) * 2 + lax.rem(zl + dl, 2))
+    for m in range(n_p):
+        for dq in range(n_q):
+            if (m, dq) != (0, 0):
+                to = (peer(m), lax.rem(q + dq, n_q))
                 pl.semaphore_signal(barrier, inc=1, device_id=to, device_id_type=MESH)
 
     def pair_rows(k):
@@ -131,46 +137,55 @@
             send[e] = turn[pl.ds(at, per * SUB), :].astype(BF16)
             return 0
 
-        lax.fori_loop(0, n_e, cast, 0, unroll=4)
-
-    def r_copy(dp, dl, arriving=False):
-        to_p, to_l = lax.rem(p + dp, n_p), lax.rem(zl + dl, 2)
+        lax.fori_loop(0, n_p, cast, 0, unroll=4)
+
+    def remote(src, dst, ss, rs, to):
         return pltpu.make_async_remote_copy(
-            src_ref=rsend.at[to_p * 2 + to_l],
-            dst_ref=rrecv.at[dl, dp],
-            send_sem=r_ss.at[dl, dp],
-            recv_sem=r_rs.at[dl, dp],
-            device_id=(to_p, zh * 2 + to_l),
-            device_id_type=MESH,
-        )
-
-    def l_copy(dp, group):
-        dh, dl = GROUPS[group]
-        to_p, to_l = lax.rem(p + dp, n_p), lax.rem(zl + dl, 2)
-        return pltpu.make_async_remote_copy(
-            src_ref=lsend.at[to_p * 2 + to_l],
-            dst_ref=lrecv.at[group, dp],
-            send_sem=l_ss.at[group, dp],
-            recv_sem=l_rs.at[group, dp],
-            device_id=(to_p, lax.rem(zh + dh, 2) * 2 + to_l),
-            device_id_type=MESH,
+            src_ref=src, dst_ref=dst, send_sem=ss, recv_sem=rs, device_id=to, device_id_type=MESH
+        )
+
+    def r_copy(m):
+        to = peer(m)
+        return remote(rsend.at[to], rrecv.at[0, m], r_ss.at[m], r_rs.at[m], (to, q))
+
+    def l_copy(m):
+        to = peer(m)
+        return remote(lsend.at[to], lrecv.at[0, m], l_ss.at[m], l_rs.at[m], (to, q))
+
+    def r_forward(m):
+        src = rsend.at[p] if m == 0 else rrecv.at[0, m]
+        return remote(src, rrecv.at[1, m], rf_ss.at[m], rf_rs.at[m], (p, partner))
+
+    mine = jnp.where(is_inner, 0, 1)
+
+    def l_forward(m):
+        src = lsend.at[p] if m == 0 else lrecv.at[0, m]
+        return remote(
+            src, lrecv.at[1 + mine, m], lf_ss.at[m], lf_rs.at[mine, m], (p, across)
+        )
+
+    def l_arrival(slot, m):
+        return remote(
+            lsend.at[p], lrecv.at[1 + slot, m], lf_ss.at[m], lf_rs.at[slot, m], (p, across)
         )
 
     for copy in brought:
         copy.wait()
     factor(rw_ref, rg_ref, rsend)
     pl.semaphore_wait(barrier, n_p * n_q - 1)
-    for dl in (1, 0):
-        for dp in range(n_p):
-            if (dp, dl) != (0, 0):
-                r_copy(dp, dl).start()
+    r_forward(0).start()
+    for m in range(1, n_p):
+        r_copy(m).start()
     factor(lw_ref, lg_ref, lsend)
-    for group in range(4):
-        for dp in range(n_p):
-            if (dp, group) != (0, 0):
-                l_copy(dp, group).start()
-    rrecv[0, 0] = rsend[me]
-    lrecv[0, 0] = lsend[me]
+
+    @pl.when(is_inner)
+    def _():
+        l_forward(0).start()
+
+    for m in range(1, n_p):
+        l_copy(m).start()
+    rrecv[0, 0] = rsend[p]
+    lrecv[0, 0] = lsend[p]
 
     def make_gate(k, _):
         gate[k] = jax.nn.sigmoid(
@@ -178,34 +193,35 @@
         )
         return 0
 
+    for m in range(1, n_p):
+        r_copy(m).wait_recv()
+        r_forward(m).start()
+        l_copy(m).wait_recv()
+
+        @pl.when(is_inner)
+        def _():
+            l_forward(m).start()
+
+    @pl.when(jnp.logical_not(is_inner))
+    def _():
+        for m in range(n_p):
+            l_forward(m).start()
+
     lax.fori_loop(0, rows, make_gate, 0, unroll=4)
-
-    for dl in (1, 0):
-        for dp in range(n_p):
-            if (dp, dl) != (0, 0):
-                r_copy(dp, dl).wait_recv()
+    for m in range(n_p):
+        r_forward(m).wait_recv()
 
     low = lax.broadcasted_iota(jnp.int32, (SUB, LANES), 1) < width
 
-    def o_copy(group, b, dl):
-        dh, gl = GROUPS[group]
-        z = lax.rem(zh + dh, 2) * 2 + lax.rem(zl + gl, 2)
-        to_p, to_l = z * 2 + b, lax.rem(zl + dl, 2)
+    def o_copy(group, z, b, dl):
+        to_p = z * 2 + b
         away = (to_p != p) if dl == 0 else None
-        return away, pltpu.make_async_remote_copy(
-            src_ref=osend.at[group, b, dl],
-            dst_ref=orecv.at[me],
-            send_sem=o_ss.at[group, b, dl],
-            recv_sem=o_rs.at[me],
-            device_id=(to_p, zh * 2 + to_l),
-            device_id_type=MESH,
-        )
-
-    for group in range(4):
-        for dp in range(n_p):
-            if (dp, group) != (0, 0):
-                l_copy(dp, group).wait_recv()
-
+        return away, remote(
+            osend.at[group, b, dl], orecv.at[p], o_ss.at[group, b, dl], o_rs.at[p],
+            (to_p, partner if dl else q),
+        )
+
+    def run_group(group, z):
         def products(d, _):
             at = pl.ds(pl.multiple_of(d * SUB, SUB), SUB)
             left = lrecv[group, :, at, :].reshape(n_p * SUB, LANES)
@@ -225,9 +241,9 @@
             return 0
 
         lax.fori_loop(0, per, products, 0, unroll=UP)
-        for b in range(2):
-            for dl in (1, 0):
-                away, copy = o_copy(group, b, dl)
+        for dl in (1, 0):
+            for b in range(2):
+                away, copy = o_copy(group, z, b, dl)
                 if away is None:
                     copy.start()
                 else:
@@ -238,26 +254,51 @@
 
                     @pl.when(jnp.logical_not(away))
                     def _():
-                        orecv[me] = osend[group, b, dl]
+                        orecv[p] = osend[group, b, dl]
+
+    def end_group(group, z):
+        for b in range(2):
+            for dl in range(2):
+                away, copy = o_copy(group, z, b, dl)
+                if away is None:
+                    copy.wait_send()
+                else:
+
+                    @pl.when(away)
+                    def _():
+                        copy.wait_send()
+
+    far = ((1, 3 - q), (2, other_end))
+    run_group(0, q)
+
+    @pl.when(is_inner)
+    def _():
+        for slot, (group, z) in enumerate(far):
+            for m in range(n_p):
+                l_arrival(slot, m).wait_recv()
+            run_group(group, z)
 
     gain = jnp.broadcast_to(gain_ref[...], (channels, channels)).T
-    for off in range(1, n_e):
-        at = lax.rem(me + off, n_e)
-        pltpu.make_async_remote_copy(
-            src_ref=osend.at[0, 0, 0],
-            dst_ref=orecv.at[at],
-            send_sem=o_ss.at[0, 0, 0],
-            recv_sem=o_rs.at[at],
-            device_id=(p, q),
-            device_id_type=MESH,
-        ).wait_recv()
+
+    def o_arrival(at):
+        return remote(
+            osend.at[0, 0, 1], orecv.at[at], o_ss.at[0, 0, 1], o_rs.at[at], (p, partner)
+        )
+
+    for m in range(1, n_p):
+        o_arrival(peer(m)).wait_recv()
+    source = jnp.where(p // 2 == end, end, inner)
+
+    @pl.when(source != q)
+    def _():
+        o_arrival(p).wait_recv()
 
     def widen(e, _):
         at = pl.multiple_of(e * per * SUB, per * SUB)
         turn[pl.ds(at, per * SUB), :] = orecv[e].astype(F32)
         return 0
 
-    lax.fori_loop(0, n_e, widen, 0, unroll=4)
+    lax.fori_loop(0, n_p, widen, 0, unroll=4)
 
     def finish(k, _):
         v = turn[pl.ds(k, channels, stride=SUB), :]
@@ -270,30 +311,23 @@
 
     lax.fori_loop(0, rows, finish, 0, unroll=UE)
 
-    for dl in range(2):
-        for dp in range(n_p):
-            if (dp, dl) != (0, 0):
-                r_copy(dp, dl).wait_send()
-    for group in range(4):
-        for dp in range(n_p):
-            if (dp, group) != (0, 0):
-                l_copy(dp, group).wait_send()
-        for b in range(2):
-            for dl in range(2):
-                away, copy = o_copy(group, b, dl)
-                if away is None:
-                    copy.wait_send()
-                else:
-
-                    @pl.when(away)
-                    def _():
-                        copy.wait_send()
+    for m in range(n_p):
+        if m > 0:
+            r_copy(m).wait_send()
+            l_copy(m).wait_send()
+        r_forward(m).wait_send()
+        l_forward(m).wait_send()
+    end_group(0, q)
+
+    @pl.when(is_inner)
+    def _():
+        for group, z in far:
+            end_group(group, z)
 
 
 def fused(n_p, n_q, pair_array, lw, rw, lg, rg, gain, ow, og):
     channels = lw.shape[1]
-    n_e = n_p * 2
-    slab = channels // n_e * SUB
+    slab = channels // n_p * SUB
     rows = pair_array.shape[0] // 2
     dma = pltpu.SemaphoreType.DMA
     return pl.pallas_call(
@@ -309,19 +343,18 @@
             pltpu.VMEM(og.shape, BF16),
             dma((8,)),
             pltpu.VMEM((channels * SUB, LANES), F32),
-            pltpu.VMEM((n_e, slab, LANES), BF16),
-            pltpu.VMEM((n_e, slab, LANES), BF16),
-            pltpu.VMEM((4, n_p, slab, LANES), BF16),
+            pltpu.VMEM((n_p, slab, LANES), BF16),
+            pltpu.VMEM((n_p, slab, LANES), BF16),
+            pltpu.VMEM((3, n_p, slab, LANES), BF16),
             pltpu.VMEM((2, n_p, slab, LANES), BF16),
-            pltpu.VMEM((4, 2, 2, slab, LANES), BF16),
-            pltpu.VMEM((n_e, slab, LANES), BF16),
+            pltpu.VMEM((3, 2, 2, slab, LANES), BF16),
+            pltpu.VMEM((n_p, slab, LANES), BF16),
             pltpu.VMEM((rows, LANES, channels), F32),
-            dma((4, n_p)),
-            dma((4, n_p)),
+            *[dma((n_p,))] * 5,
             dma((2, n_p)),
-            dma((2, n_p)),
-            dma((4, 2, 2)),
-            dma((n_e,)),
+            *[dma((n_p,))] * 2,
+            dma((3, 2, 2)),
+            dma((n_p,)),
         ],
         compiler_params=pltpu.CompilerParams(
             collective_id=0, has_side_effects=True, vmem_limit_bytes=67_043_328

time: 42.2 us -> 50.6 us (1.20)
  Pallas kernels: 40.2 us -> 48.5 us
    pallas_call x1, Pallas kernels: 40.2 us -> 48.5 us  [fused(): pl.pallas_call(functools.partial(kernel, n_p, n_q), out_shape=jax.ShapeDt...]
where the time goes in v3:
time: 50.6 us; the launch traced here: 50.4 us
  Pallas kernels  48.5 us (96%)
  local copies, waits for them, and re-layouts  1.87 us (4%)
    pallas_call x1, Pallas kernels, fused(): pl.pallas_call(functools.partial(kernel, n_p, n_q), out_shape=jax.ShapeDt...  48.5 us
    unnamed x1, local copies, waits for them, and re-layouts  1.87 us

profile of v3, /device:TPU:7, one launch (start us, length us, event | category | flops | bytes accessed | tf_op | source)
XLA Modules:
  0.0 50.4 jit_solution(13439854428516583672)
XLA Ops:
  0.0 48.5 %shard_map.82 = bf16[32,64,128]{2,1,0:T(8,128)(2,1)} custom-call(bf16[32,64,128]{2,1,0:T(8,128)(2,1)} %x_hbm.1, bf16[128,128]{1,0:T(8,128)(2,1)} %lw_hbm.1, bf16[128,128]{1,0:T(8,128)(2,1)} %rw_hbm.1, bf16[128,128]{1,0:T(8,128)(2,1)} %lg_hbm.1, bf16[128,128]{1,0:T(8,128)(2,1)} %rg_hbm.1, f32[1,128]{1,0:T(1,128)} %bitcast.1, bf16[128,128]{1,0:T(8,128)(2,1)} %ow_hbm.1, ...), custom_call_target="tpu_custom_call" | custom-call | tf_op jit(solution)/shard_map/pallas_call | solution.py:333
  48.5 1.9 %copy.10 = bf16[32,64,128]{2,1,0:T(8,128)(2,1)} copy(bf16[32,64,128]{2,1,0:T(8,128)(2,1)} %shard_map.82) | data formatting | bytes 1048576
